TPU v7x, 256 devices: a whole 4x4x8 slice. The times are simulated.
256 devices in a mesh: pop: 64 (over x, z, core), mp: 4 (over y).
Axes of the slice: x: 4, y: 4, z: 8, core: 2. Of those that a mesh axis runs over, the one named last changes fastest.
Arguments:
- tokens: bfloat16 [256, 3584], replicated, may hold values from -60 to 60
- target: bfloat16 [256, 3584], P(None, 'mp'), may hold values from -6 to 6
- w_query: bfloat16 [3584, 3584], P('pop', 'mp'), may hold values from -0.09375 to 0.09375
- w_key: bfloat16 [3584, 512], P(None, 'mp'), may hold values from -0.09375 to 0.09375
- w_value: bfloat16 [3584, 512], P(None, 'mp'), may hold values from -0.09375 to 0.09375
- w_out: bfloat16 [3584, 3584], P('mp', 'pop'), may hold values from -0.09375 to 0.09375
- query_left_factors: bfloat16 [64, 3584, 4], P('pop'), may hold values from -0.09375 to 0.09375
- query_right_factors: bfloat16 [64, 4, 3584], P('pop', None, 'mp'), may hold values from -6 to 6
- o_left: bfloat16 [64, 3584, 4], P('pop', 'mp'), may hold values from -0.09375 to 0.09375
- o_right: bfloat16 [64, 4, 3584], P('pop'), may hold values from -6 to 6
- member_ids: int32 [64], P('pop'), may hold values from 0 to 63, each once
Outputs:
- grad_query: float32 [3584, 3584], P('pop', 'mp')
- grad_out: float32 [3584, 3584], P('mp', 'pop')
- fitness: float32 [64], P('pop')
Inputs may be any that keep to these rules, and one draw needn't show every extreme that they name: `member_ids`: every number from 0 to 63 appears once.
All inputs are finite; a program needn't handle non-finite values.
Results may differ from a plain program's by a relative error of at most 0.005.
Values may be sent and summed in bfloat16 or wider, within the bound.
No kernel may reach another device: no remote copies, remote signals or barrier semaphores. Data moves between devices by JAX's collectives and lax.ppermute only.
A program may use at most 64 MiB of HBM per device.

v0:
```python
import math
import jax
import jax.numpy as jnp
from jax import lax
from jax.sharding import Mesh
from jax.sharding import PartitionSpec as P

D = 3584
HEADS = 28
KV_HEADS = 4
HEAD_DIM = 128
RANK = 4
POP = ("pop_0", "pop_1", "pop_2")
noise_scale = 0.5
rope_base = 1000000.0
spread_floor = 0.001


def in_order(parts, dim):
    parts = jnp.moveaxis(parts, 0, dim)
    shape = parts.shape
    return parts.reshape(*shape[:dim], shape[dim] * shape[dim + 1], *shape[dim + 2 :])


def all_blocks(shard, axes, turns):
    parts = shard[None]
    for k in turns:
        parts = lax.all_gather(parts, axes[k], axis=0, tiled=True)
    held = [lax.axis_size(axes[k]) for k in reversed(turns)]
    parts = parts.reshape(*held, *shard.shape)
    turned = sorted(range(len(turns)), key=lambda place: turns[len(turns) - 1 - place])
    return parts.transpose(*turned, *range(len(turns), parts.ndim)).reshape(-1, *shard.shape)


def whole_of(shard, axes, turns, dim):
    return in_order(all_blocks(shard, axes, turns), dim)


def cut_along(shard, dim, devices):
    before, after = (shard.shape[:dim], shard.shape[dim + 1 :])
    return jnp.moveaxis(shard.reshape(*before, devices, -1, *after), dim, 0)


def summed_on_arrival(shard, axis, dim):
    devices = lax.axis_size(axis)
    parts = lax.all_to_all(cut_along(shard, dim, devices), axis, 0, 0, tiled=True)
    return jnp.sum(parts.astype(jnp.float32), axis=0)


def copy_for_each(shard, axis):
    copies = jnp.broadcast_to(shard, (lax.axis_size(axis), *shard.shape))
    return lax.all_to_all(copies, axis, split_axis=0, concat_axis=0, tiled=True)


def of_everyone(shard, axis):
    return copy_for_each(shard, axis).sum(axis=0)


def gathered_copies(shard, axis, dim):
    return in_order(copy_for_each(shard, axis), dim)


def side_by_side(arrays, axis, dim, along):
    columns = [a.reshape(*a.shape[:along], -1) for a in arrays]
    both = jnp.concatenate(columns, axis=along)
    result, at, done = (lax.all_gather(both, axis, axis=dim, tiled=True), 0, [])
    for a, column in zip(arrays, columns):
        share = result[..., at : at + column.shape[along]]
        done.append(share.reshape(*share.shape[:along], *a.shape[along:]))
        at += column.shape[along]
    return tuple(done)


def tables(count, head_size):
    position = jnp.arange(count, dtype=jnp.float32)
    index = jnp.arange(head_size // 2, dtype=jnp.float32)
    freq = jnp.exp(-math.log(rope_base) * 2.0 * index / head_size)
    angle = position[:, None] * freq[None, :]
    return (jnp.cos(angle)[:, None, :], jnp.sin(angle)[:, None, :])


def rotate(field, cosine_table, sine):
    half = field.shape[-1] // 2
    first = field[..., :half]
    second = field[..., half:]
    return jnp.concatenate(
        [first * cosine_table - second * sine, second * cosine_table + first * sine], axis=-1
    )


def per_device(
    tokens,
    target,
    w_query,
    w_key,
    w_value,
    w_out,
    query_left_factors,
    query_right_factors,
    o_left,
    o_right,
    member_ids,
):
    tok = tokens.shape[0]
    local_feats = w_query.shape[1]
    local_kv = w_key.shape[1] // HEAD_DIM
    group = HEADS // KV_HEADS
    local_heads = local_kv * group
    slots = query_left_factors.shape[0]
    scale = HEAD_DIM ** (-0.5)
    cosine_table, sine = tables(tok, HEAD_DIM)
    base = jnp.dot(tokens, whole_of(w_query, POP, (0, 1, 2), 0), preferred_element_type=jnp.float32)
    keys = rotate(
        jnp.dot(tokens, w_key, preferred_element_type=jnp.float32).reshape(tok, local_kv, HEAD_DIM),
        cosine_table,
        sine,
    ).astype(jnp.bfloat16)
    values = (
        jnp.dot(tokens, w_value, preferred_element_type=jnp.float32)
        .astype(jnp.bfloat16)
        .reshape(tok, local_kv, HEAD_DIM)
    )
    signs = (1 - 2 * (member_ids % 2)).astype(jnp.float32)
    factor = noise_scale * signs[:, None, None]
    lowrank_product = jnp.einsum(
        "td,mdr->mtr", tokens, query_left_factors, preferred_element_type=jnp.float32
    ).astype(jnp.bfloat16)
    query = base[None] + factor * jnp.einsum(
        "olj,ojv->olv", lowrank_product, query_right_factors, preferred_element_type=jnp.float32
    )
    query = rotate(
        query.reshape(slots, tok, local_heads, HEAD_DIM), cosine_table[None], sine[None]
    ).astype(jnp.bfloat16)
    query = query.reshape(slots, tok, local_kv, group, HEAD_DIM)
    scores = jnp.einsum("mtkgd,skd->mkgts", query, keys, preferred_element_type=jnp.float32) * scale
    causal = jnp.arange(tok)[:, None] >= jnp.arange(tok)[None, :]
    scores = jnp.where(causal, scores, -1e30)
    probs = jax.nn.softmax(scores, axis=-1).astype(jnp.bfloat16)
    mixed = (
        jnp.einsum("mkgts,skd->mtkgd", probs, values, preferred_element_type=jnp.float32)
        .astype(jnp.bfloat16)
        .reshape(slots, tok, local_feats)
    )
    low_out = jnp.einsum("mtf,mfr->mtr", mixed, o_left, preferred_element_type=jnp.float32)
    right_full = o_right.astype(jnp.float32)
    part = jnp.einsum(
        "mtf,fe->mte",
        mixed,
        lax.all_gather(w_out, POP, axis=1, tiled=True),
        preferred_element_type=jnp.float32,
    )
    term = part + factor * jnp.einsum(
        "mtr,mre->mte", low_out, right_full, precision=lax.Precision.HIGHEST
    )
    output = summed_on_arrival(term.astype(jnp.bfloat16), "mp", 2)
    diff = output - target.astype(jnp.float32)[None]
    errors = of_everyone(jnp.sum(diff * diff, axis=(1, 2)), "mp")
    fitness = -(errors / (tok * D))
    count = slots * lax.axis_size(POP)
    everyone = gathered_copies(fitness, POP, 0)
    mean = jnp.sum(everyone) / count
    spread = jnp.sum((everyone - mean) * (everyone - mean)) / count
    weight = signs * (fitness - mean) / jnp.sqrt(spread + spread_floor)
    every_weight = gathered_copies(weight, POP, 0)
    right_factors_gathered, left_all = side_by_side((query_right_factors, o_left), POP, 0, 1)
    rows_q = lax.all_to_all(query_left_factors, POP, split_axis=1, concat_axis=0, tiled=True)
    cols_o = lax.all_to_all(o_right, POP, split_axis=2, concat_axis=0, tiled=True)
    whole_population = rows_q.shape[0]
    left_q = jnp.transpose(
        rows_q.astype(jnp.float32) * every_weight[:, None, None], (1, 0, 2)
    ).reshape(rows_q.shape[1], whole_population * RANK)
    right_q = right_factors_gathered.astype(jnp.float32).reshape(
        whole_population * RANK, local_feats
    )
    grad_query = jnp.dot(left_q, right_q, precision=lax.Precision.HIGHEST) / noise_scale
    output_left_factor = jnp.transpose(
        left_all.astype(jnp.float32) * every_weight[:, None, None], (1, 0, 2)
    ).reshape(local_feats, whole_population * RANK)
    right_o = cols_o.astype(jnp.float32).reshape(whole_population * RANK, cols_o.shape[2])
    grad_out = jnp.dot(output_left_factor, right_o, precision=lax.Precision.HIGHEST) / noise_scale
    return (grad_query, grad_out, fitness)


def solution(mesh):
    torus = Mesh(mesh.devices.reshape(4, 8, 2, mesh.shape["mp"]), ("pop_0", "pop_1", "pop_2", "mp"))
    placed = (
        P(),
        P(None, "mp"),
        P(POP, "mp"),
        P(None, "mp"),
        P(None, "mp"),
        P("mp", POP),
        P(POP, None, None),
        P(POP, None, "mp"),
        P(POP, "mp", None),
        P(POP, None, None),
        P(POP),
    )
    return jax.shard_map(
        per_device,
        mesh=torus,
        in_specs=placed,
        out_specs=(P(POP, "mp"), P("mp", POP), P(POP)),
        check_vma=False,
    )
```

profile of v0, /device:TPU:1, one launch (start us, length us, event | category | flops | bytes accessed | tf_op | source)
XLA Modules:
  0.0 428.7 jit_solution(7784847421207332163)
XLA Ops:
  7.2 13.0 %all-gather = bf16[224,896]{1,0:T(8,128)(2,1)} all-gather(bf16[56,896]{1,0:T(8,128)(2,1)} %param.13), channel_id=2, replica_groups=mesh['pop_0'=4,'pop_1'=8,'pop_2'=2,'mp'=4] {'pop_0'}, dimensions={0}, use_global_device_ids=true | all-gather | bytes 501760 | tf_op jit(solution)/shard_map/all_gather | solution.py:28
  20.3 49.6 %all-gather.6.cloned.1.call-done = bf16[32,56,896]{2,1,0:T(8,128)(2,1)} async-done(((bf16[4,56,896]{2,1,0:T(8,128)(2,1)}), bf16[32,56,896]{2,1,0:T(8,128)(2,1)}) %all-gather.6.cloned.1.call-update) | async-done | bytes 3211280 | tf_op jit(solution)/shard_map/all_gather | solution.py:28
  70.0 0.7 all-gather.10.cloned.1.call-update
  71.4 0.7 convolution_bitcast_fusion
  72.2 1.0 fusion.18
  73.6 19.9 %all-gather.8.cloned.1.call-done = bf16[64,56,896]{2,1,0:T(8,128)(2,1)} async-done(((bf16[32,56,896]{2,1,0:T(8,128)(2,1)}), bf16[64,56,896]{2,1,0:T(8,128)(2,1)}) %all-gather.8.cloned.1.call-update) | async-done | bytes 6422544 | tf_op jit(solution)/shard_map/all_gather | solution.py:28
  93.5 3.3 copy.114
  96.9 2.1 fusion.29
  99.1 2.1 fusion.3
  101.1 1.5 copy.115
  102.6 0.9 fusion.27
  103.5 1.3 copy.140
  104.8 1.3 copy.141
  106.1 1.4 fusion.7
  108.2 1.2 copy-done.2
  110.0 2.6 convolution_convert_fusion
  112.8 65.1 %all-gather.10.cloned.1.call-done = bf16[896,3584]{0,1:T(8,128)(2,1)} async-done(((bf16[896,56]{0,1:T(8,128)(2,1)}), bf16[896,3584]{0,1:T(8,128)(2,1)}) %all-gather.10.cloned.1.call-update) | async-done | bytes 6422544 | tf_op jit(solution)/shard_map/all_gather | solution.py:149
  177.9 4.9 %fusion.30 = f32[256,3584]{1,0:T(8,128)S(1)} fusion(bf16[256,896]{0,1:T(8,128)(2,1)S(1)} %bitcast.106, bf16[896,3584]{0,1:T(8,128)(2,1)} %all-gather.10.cloned.1.call-done), kind=kOutput, calls=%fused_computation.58 | convolution fusion | flops 1644167168 | bytes 10551296 | tf_op jit(solution)/shard_map/mtf,fe->mte/dot_general | solution.py:146
  182.8 3.1 fusion.1
  185.9 3.3 reshape.288
  189.2 1.5 copy.145
  190.7 4.0 all-to-all-start.1
  195.3 22.5 %all-to-all-done.1 = bf16[4,1,256,896]{3,2,1,0:T(8,128)(2,1)S(1)} async-done(((bf16[4,1,256,896]{3,2,1,0:T(8,128)(2,1)}), bf16[4,1,256,896]{3,2,1,0:T(8,128)(2,1)S(1)}, u32[]{:S(2)}, u32[]{:S(2)}) %all-to-all-start.1) | async-done | bytes 1835040 | tf_op jit(solution)/shard_map/all_to_all | solution.py:46
  218.1 0.9 multiply_reduce_fusion
  218.9 0.6 broadcast_in_dim.34
  219.6 6.5 %all_to_all.47 = f32[4,1,1]{2,1,0:T(1,128)S(1)} all-to-all(f32[4,1,1]{2,1,0:T(1,128)S(1)} %broadcast_in_dim.34), channel_id=1, replica_groups=mesh['pop_0'=4,'pop_1'=8,'pop_2'=2,'mp'=4] {'mp'}, dimensions={0} | all-to-all | bytes 32 | tf_op jit(solution)/shard_map/all_to_all | solution.py:52
  227.3 0.6 broadcast_in_dim.35
  227.9 7.9 %all-to-all-start.3 = ((f32[64,1,1]{2,1,0:T(1,128)}), f32[64,1,1]{2,1,0:T(1,128)S(1)}, u32[]{:S(2)}, u32[]{:S(2)}) async-start(f32[64,1,1]{2,1,0:T(1,128)} %broadcast_in_dim.35), calls=%async_computation.3 | async-start | bytes 65536 | tf_op jit(solution)/shard_map/all_to_all | solution.py:52
  235.9 51.8 %all-gather.1 = bf16[64,1,7168]{2,1,0:T(2,128)(2,1)S(1)} all-gather(bf16[1,1,7168]{2,1,0:T(2,128)(2,1)S(1)} %maximum_bitcast_fusion.2), channel_id=1, replica_groups=mesh['pop_0'=4,'pop_1'=8,'pop_2'=2,'mp'=4] {'pop_0','pop_1','pop_2'}, dimensions={0}, use_global_device_ids=true | all-gather | bytes 931840 | tf_op jit(solution)/shard_map/all_gather | solution.py:66
  287.7 3.2 copy.129
  290.9 1.2 copy.146
  292.2 7.3 %all-to-all-start.5 = ((bf16[1,4,3584]{1,0,2:T(2,128)(2,1)}), bf16[1,4,3584]{1,0,2:T(2,128)(2,1)S(1)}, u32[]{:S(2)}, u32[]{:S(2)}) async-start(bf16[1,4,3584]{1,0,2:T(2,128)(2,1)} %copy.129), calls=%async_computation.5 | async-start | bytes 3670016 | tf_op jit(solution)/shard_map/all_to_all | solution.py:167
  299.4 2.0 slice_convert_fusion
  301.5 3.2 copy.112
  304.7 0.7 reduce_sum.58
  306.1 38.7 %all-to-all-done.5 = bf16[1,4,3584]{1,0,2:T(2,128)(2,1)S(1)} async-done(((bf16[1,4,3584]{1,0,2:T(2,128)(2,1)}), bf16[1,4,3584]{1,0,2:T(2,128)(2,1)S(1)}, u32[]{:S(2)}, u32[]{:S(2)}) %all-to-all-start.5) | async-done | bytes 28704 | tf_op jit(solution)/shard_map/all_to_all | solution.py:167
  344.8 6.2 %all-to-all-start = ((bf16[1,3584,4]{2,0,1:T(2,128)(2,1)}), bf16[1,3584,4]{2,0,1:T(2,128)(2,1)}, u32[]{:S(2)}, u32[]{:S(2)}) async-start(bf16[1,3584,4]{2,0,1:T(2,128)(2,1)} %copy.112), calls=%async_computation | async-start | bytes 3670016 | tf_op jit(solution)/shard_map/all_to_all | solution.py:166
  352.3 44.0 %all-to-all-done = bf16[1,3584,4]{2,0,1:T(2,128)(2,1)} async-done(((bf16[1,3584,4]{2,0,1:T(2,128)(2,1)}), bf16[1,3584,4]{2,0,1:T(2,128)(2,1)}, u32[]{:S(2)}, u32[]{:S(2)}) %all-to-all-start) | async-done | bytes 28704 | tf_op jit(solution)/shard_map/all_to_all | solution.py:166
  396.9 6.0 %all-to-all-start.4 = ((f32[64,1,1]{2,1,0:T(1,128)}), f32[64,1,1]{2,1,0:T(1,128)S(1)}, u32[]{:S(2)}, u32[]{:S(2)}) async-start(f32[64,1,1]{2,1,0:T(1,128)} %broadcast_in_dim.36), calls=%async_computation.4 | async-start | bytes 65536 | tf_op jit(solution)/shard_map/all_to_all | solution.py:52
  403.0 1.8 copy.127
  404.7 1.3 reshape.292
  406.0 1.8 copy.130
  408.1 3.7 copy.113
  412.8 1.6 multiply_bitcast_fusion
  414.4 2.8 copy.128
  417.2 1.5 reshape.293
  418.9 1.1 convolution_multiply_fusion.3
  420.0 1.1 convolution_multiply_fusion.2
  (55 shorter events, 6.1 us)
Async XLA Ops:
  7.2 64.2 %copy-start = (bf16[256,3584]{1,0:T(8,128)(2,1)S(1)}, bf16[256,3584]{1,0:T(8,128)(2,1)}, u32[]{:S(2)}) copy-start(bf16[256,3584]{1,0:T(8,128)(2,1)} %param.11) | copy-start | bytes 5505028
  7.2 62.7 %all-gather.6.cloned.1.call-start = ((), (), s32[]{:S(2)}) async-start(), calls=%async_computation.6 | async-start | bytes 3612672 | tf_op jit(solution)/shard_map/all_gather | solution.py:28
  20.2 51.2 %copy-start.4 = (bf16[3584,128]{1,0:T(8,128)(2,1)S(1)}, bf16[3584,128]{1,0:T(8,128)(2,1)}, u32[]{:S(2)}) copy-start(bf16[3584,128]{1,0:T(8,128)(2,1)} %param.14) | copy-start | bytes 2752516
  20.3 73.3 %all-gather.8.cloned.1.call-start = ((), (), s32[]{:S(2)}) async-start(), calls=%async_computation.7 | async-start | bytes 9633792 | tf_op jit(solution)/shard_map/all_gather | solution.py:28
  69.9 107.9 %all-gather.10.cloned.1.call-start = ((), (), s32[]{:S(2)}) async-start(), calls=%async_computation.8 | async-start | bytes 6522880 | tf_op jit(solution)/shard_map/all_gather | solution.py:149
  96.9 2.2 copy-start.9
  96.9 2.2 copy-start.11
  106.1 1.4 copy-start.6
  106.1 1.4 copy-start.7
  108.1 1.3 copy-start.2
  108.2 1.9 copy-start.13
  110.0 2.6 copy-start.12
  112.8 70.0 %copy-start.8 = (bf16[1,4,3584]{2,1,0:T(4,128)(2,1)S(1)}, bf16[1,4,3584]{2,1,0:T(4,128)(2,1)}, u32[]{:S(2)}) copy-start(bf16[1,4,3584]{2,1,0:T(4,128)(2,1)} %param.20) | copy-start | bytes 86020
  190.7 27.1 %all-to-all-start.1 = ((bf16[4,1,256,896]{3,2,1,0:T(8,128)(2,1)}), bf16[4,1,256,896]{3,2,1,0:T(8,128)(2,1)S(1)}, u32[]{:S(2)}, u32[]{:S(2)}) async-start(bf16[4,1,256,896]{3,2,1,0:T(8,128)(2,1)} %bitcast.98), calls=%async_computation.1 | async-start | bytes 3670016 | tf_op jit(solution)/shard_map/all_to_all | solution.py:46
  194.7 23.3 %copy-start.5 = (bf16[256,896]{1,0:T(8,128)(2,1)S(1)}, bf16[256,896]{1,0:T(8,128)(2,1)}, u32[]{:S(2)}) copy-start(bf16[256,896]{1,0:T(8,128)(2,1)} %param.12) | copy-start | bytes 1376260
  227.9 64.2 %all-to-all-start.3 = ((f32[64,1,1]{2,1,0:T(1,128)}), f32[64,1,1]{2,1,0:T(1,128)S(1)}, u32[]{:S(2)}, u32[]{:S(2)}) async-start(f32[64,1,1]{2,1,0:T(1,128)} %broadcast_in_dim.35), calls=%async_computation.3 | async-start | bytes 65536 | tf_op jit(solution)/shard_map/all_to_all | solution.py:52
  292.2 52.6 %all-to-all-start.5 = ((bf16[1,4,3584]{1,0,2:T(2,128)(2,1)}), bf16[1,4,3584]{1,0,2:T(2,128)(2,1)S(1)}, u32[]{:S(2)}, u32[]{:S(2)}) async-start(bf16[1,4,3584]{1,0,2:T(2,128)(2,1)} %copy.129), calls=%async_computation.5 | async-start | bytes 3670016 | tf_op jit(solution)/shard_map/all_to_all | solution.py:167
  299.4 2.1 copy-start.10
  344.8 51.5 %all-to-all-start = ((bf16[1,3584,4]{2,0,1:T(2,128)(2,1)}), bf16[1,3584,4]{2,0,1:T(2,128)(2,1)}, u32[]{:S(2)}, u32[]{:S(2)}) async-start(bf16[1,3584,4]{2,0,1:T(2,128)(2,1)} %copy.112), calls=%async_computation | async-start | bytes 3670016 | tf_op jit(solution)/shard_map/all_to_all | solution.py:166
  396.9 15.3 %all-to-all-start.4 = ((f32[64,1,1]{2,1,0:T(1,128)}), f32[64,1,1]{2,1,0:T(1,128)S(1)}, u32[]{:S(2)}, u32[]{:S(2)}) async-start(f32[64,1,1]{2,1,0:T(1,128)} %broadcast_in_dim.36), calls=%async_computation.4 | async-start | bytes 65536 | tf_op jit(solution)/shard_map/all_to_all | solution.py:52
  407.9 4.9 %copy-start.3 = (f32[64,3584]{0,1:T(8,128)S(1)}, f32[64,3584]{0,1:T(8,128)}, u32[]{:S(2)}) copy-start(f32[64,3584]{0,1:T(8,128)} %copy.127) | copy-start | bytes 2752516
  414.3 6.7 %copy-start.1 = (bf16[256,3584]{1,0:T(8,128)(2,1)S(1)}, bf16[256,3584]{1,0:T(8,128)(2,1)}, u32[]{:S(2)}) copy-start(bf16[256,3584]{1,0:T(8,128)(2,1)} %param.11) | copy-start | bytes 5505028
Sparse Core Ops, SparseCore 0:
  20.4 49.4 all-gather.5
  71.7 21.7 all-gather.7
  96.2 81.5 all-gather.9
where the time goes:
time: 430 us; the launch traced here: 429 us
  waiting for transfers between devices  241 us (56%)
  blocking collectives  71.3 us (17%)
  local copies, waits for them, and re-layouts  38.2 us (9%)
  starting transfers between devices  31.5 us (7%)
  matrix products  18.6 us (4%)
  between operations  17.9 us (4%)
  other arithmetic  10.5 us (2%)
    all_gather x2, waiting for transfers between devices, all_blocks(): parts = lax.all_gather(parts, axes[k], axis=0, tiled=True)  69.5 us
    all_gather x1, waiting for transfers between devices, per_device(): lax.all_gather(w_out, POP, axis=1, tiled=True)  65.1 us
    all_gather x1, blocking collectives, side_by_side(): result, at, done = (lax.all_gather(both, axis, axis=dim, tiled=True), 0, [])  51.8 us
    all_to_all x1, waiting for transfers between devices, per_device(): lax.all_to_all(query_left_factors, POP, split_axis=1, concat_axis=0, tile...  44 us
    all_to_all x1, waiting for transfers between devices, per_device(): lax.all_to_all(o_right, POP, split_axis=2, concat_axis=0, tiled=True)  38.7 us
    all_to_all x1, waiting for transfers between devices, summed_on_arrival(): lax.all_to_all(cut_along(shard, dim, devices), axis, 0, 0, tiled=True)  22.5 us
    all_to_all x2, starting transfers between devices, copy_for_each(): return lax.all_to_all(copies, axis, split_axis=0, concat_axis=0, tiled=True)  14 us
    all_gather x1, blocking collectives, all_blocks(): parts = lax.all_gather(parts, axes[k], axis=0, tiled=True)  13 us
  transfers between devices with their start and end apart: 8, of which 7 were waited for; matrix products, arithmetic and copies ran while one was open for 9% of the time, Pallas kernels for 0%

commit v1 on v0

--- a/solution.py
+++ b/solution.py
@@ -146,7 +146,7 @@
     part = jnp.einsum(
         "mtf,fe->mte",
         mixed,
-        lax.all_gather(w_out, POP, axis=1, tiled=True),
+        jnp.concatenate(lax.all_to_all(jnp.stack([w_out] * lax.axis_size(POP)), POP, 0, 0), axis=1),
         preferred_element_type=jnp.float32,
     )
     term = part + factor * jnp.einsum(

time: 430 us -> 462 us (1.074)
  waiting for transfers between devices: 241 us -> 255 us
  starting transfers between devices: 31.5 us -> 44.8 us
    all_gather x1 -> x0, waiting for transfers between devices: 65.1 us -> none  [per_device(): lax.all_gather(w_out, POP, axis=1, tiled=True)]
    all_gather x2, waiting for transfers between devices: 69.5 us -> 128 us  [all_blocks(): parts = lax.all_gather(parts, axes[k], axis=0, tiled=True)]
    all_to_all x0 -> x1, waiting for transfers between devices: none -> 21.6 us  [per_device(): lax.all_to_all(jnp.stack([w_out] * lax.axis_size(POP)), POP, 0, 0)]
    all_to_all x0 -> x1, starting transfers between devices: none -> 13.5 us  [per_device(): lax.all_to_all(jnp.stack([w_out] * lax.axis_size(POP)), POP, 0, 0)]
  transfers between devices with their start and end apart: 8 -> 8, of which waited for: 7 -> 7; matrix products, arithmetic and copies ran while one was open for 9% -> 10% of each run, Pallas kernels for 0% -> 0%
where the time goes in v1:
time: 462 us; the launch traced here: 461 us
  waiting for transfers between devices  255 us (55%)
  blocking collectives  71.3 us (15%)
  starting transfers between devices  44.8 us (10%)
  local copies, waits for them, and re-layouts  42.4 us (9%)
  matrix products  18.6 us (4%)
  between operations  18.3 us (4%)
  other arithmetic  10.5 us (2%)
    all_gather x2, waiting for transfers between devices, all_blocks(): parts = lax.all_gather(parts, axes[k], axis=0, tiled=True)  128 us
    all_gather x1, blocking collectives, side_by_side(): result, at, done = (lax.all_gather(both, axis, axis=dim, tiled=True), 0, [])  51.8 us
    all_to_all x1, waiting for transfers between devices, per_device(): lax.all_to_all(query_left_factors, POP, split_axis=1, concat_axis=0, tile...  44 us
    all_to_all x1, waiting for transfers between devices, per_device(): lax.all_to_all(o_right, POP, split_axis=2, concat_axis=0, tiled=True)  38.8 us
    all_to_all x1, waiting for transfers between devices, summed_on_arrival(): lax.all_to_all(cut_along(shard, dim, devices), axis, 0, 0, tiled=True)  22.4 us
    all_to_all x1, waiting for transfers between devices, per_device(): lax.all_to_all(jnp.stack([w_out] * lax.axis_size(POP)), POP, 0, 0)  21.6 us
    all_to_all x2, starting transfers between devices, copy_for_each(): return lax.all_to_all(copies, axis, split_axis=0, concat_axis=0, tiled=True)  13.8 us
    all_to_all x1, starting transfers between devices, per_device(): lax.all_to_all(jnp.stack([w_out] * lax.axis_size(POP)), POP, 0, 0)  13.5 us
  transfers between devices with their start and end apart: 8, of which 7 were waited for; matrix products, arithmetic and copies ran while one was open for 10% of the time, Pallas kernels for 0%

profile of v1, /device:TPU:1, one launch (start us, length us, event | category | flops | bytes accessed | tf_op | source)
XLA Modules:
  0.0 460.7 jit_solution(10587158637562555518)
XLA Ops:
  7.2 13.0 %all-gather = bf16[224,896]{1,0:T(8,128)(2,1)} all-gather(bf16[56,896]{1,0:T(8,128)(2,1)} %param.13), channel_id=2, replica_groups=mesh['pop_0'=4,'pop_1'=8,'pop_2'=2,'mp'=4] {'pop_0'}, dimensions={0}, use_global_device_ids=true | all-gather | bytes 501760 | tf_op jit(solution)/shard_map/all_gather | solution.py:28
  20.3 4.0 stack.2
  24.3 13.5 %all-to-all-start.1 = ((bf16[64,896,56]{1,2,0:T(8,128)(2,1)}), bf16[64,896,56]{1,2,0:T(8,128)(2,1)}, u32[]{:S(2)}, u32[]{:S(2)}) async-start(bf16[64,896,56]{1,2,0:T(8,128)(2,1)} %stack.2), calls=%async_computation.1 | async-start | bytes 12845056 | tf_op jit(solution)/shard_map/all_to_all | solution.py:149
  37.8 104.5 %all-gather.5.cloned.1.call-done = bf16[32,56,896]{2,1,0:T(8,128)(2,1)} async-done(((bf16[4,56,896]{2,1,0:T(8,128)(2,1)}), bf16[32,56,896]{2,1,0:T(8,128)(2,1)}) %all-gather.5.cloned.1.call-update) | async-done | bytes 3211280 | tf_op jit(solution)/shard_map/all_gather | solution.py:28
  143.1 0.7 convolution_bitcast_fusion
  143.9 1.0 fusion.18
  145.3 23.5 %all-gather.7.cloned.1.call-done = bf16[64,56,896]{2,1,0:T(8,128)(2,1)} async-done(((bf16[32,56,896]{2,1,0:T(8,128)(2,1)}), bf16[64,56,896]{2,1,0:T(8,128)(2,1)}) %all-gather.7.cloned.1.call-update) | async-done | bytes 6422544 | tf_op jit(solution)/shard_map/all_gather | solution.py:28
  168.8 3.3 copy.115
  172.2 2.1 fusion.29
  174.4 2.1 fusion.3
  176.5 1.5 copy.116
  178.0 0.9 fusion.27
  178.9 1.3 copy.141
  180.2 1.3 copy.142
  181.5 1.4 fusion.7
  183.6 1.2 copy-done.2
  185.5 2.6 convolution_convert_fusion
  188.2 21.6 %all-to-all-done.1 = bf16[64,896,56]{1,2,0:T(8,128)(2,1)} async-done(((bf16[64,896,56]{1,2,0:T(8,128)(2,1)}), bf16[64,896,56]{1,2,0:T(8,128)(2,1)}, u32[]{:S(2)}, u32[]{:S(2)}) %all-to-all-start.1) | async-done | bytes 6422560 | tf_op jit(solution)/shard_map/all_to_all | solution.py:149
  209.8 4.9 %fusion.30 = f32[256,3584]{1,0:T(8,128)S(1)} fusion(bf16[256,896]{0,1:T(8,128)(2,1)S(1)} %bitcast.109, bf16[896,3584]{0,1:T(8,128)(2,1)} %bitcast.25), kind=kOutput, calls=%fused_computation.58 | convolution fusion | flops 1644167168 | bytes 10551296 | tf_op jit(solution)/shard_map/mtf,fe->mte/dot_general | solution.py:146
  214.7 3.1 fusion.1
  217.8 3.3 reshape.298
  221.2 1.5 copy.146
  222.7 4.0 all-to-all-start.2
  227.2 22.4 %all-to-all-done.2 = bf16[4,1,256,896]{3,2,1,0:T(8,128)(2,1)S(1)} async-done(((bf16[4,1,256,896]{3,2,1,0:T(8,128)(2,1)}), bf16[4,1,256,896]{3,2,1,0:T(8,128)(2,1)S(1)}, u32[]{:S(2)}, u32[]{:S(2)}) %all-to-all-start.2) | async-done | bytes 1835040 | tf_op jit(solution)/shard_map/all_to_all | solution.py:46
  249.9 0.9 multiply_reduce_fusion
  250.7 0.6 broadcast_in_dim.34
  251.4 6.5 %all_to_all.52 = f32[4,1,1]{2,1,0:T(1,128)S(1)} all-to-all(f32[4,1,1]{2,1,0:T(1,128)S(1)} %broadcast_in_dim.34), channel_id=1, replica_groups=mesh['pop_0'=4,'pop_1'=8,'pop_2'=2,'mp'=4] {'mp'}, dimensions={0} | all-to-all | bytes 32 | tf_op jit(solution)/shard_map/all_to_all | solution.py:52
  259.8 7.8 %all-to-all-start.4 = ((f32[64,1,1]{2,1,0:T(1,128)}), f32[64,1,1]{2,1,0:T(1,128)S(1)}, u32[]{:S(2)}, u32[]{:S(2)}) async-start(f32[64,1,1]{2,1,0:T(1,128)} %broadcast_in_dim.35), calls=%async_computation.4 | async-start | bytes 65536 | tf_op jit(solution)/shard_map/all_to_all | solution.py:52
  267.5 51.8 %all-gather.1 = bf16[64,1,7168]{2,1,0:T(2,128)(2,1)S(1)} all-gather(bf16[1,1,7168]{2,1,0:T(2,128)(2,1)S(1)} %maximum_bitcast_fusion.2), channel_id=1, replica_groups=mesh['pop_0'=4,'pop_1'=8,'pop_2'=2,'mp'=4] {'pop_0','pop_1','pop_2'}, dimensions={0}, use_global_device_ids=true | all-gather | bytes 931840 | tf_op jit(solution)/shard_map/all_gather | solution.py:66
  319.4 3.2 copy.130
  322.6 1.2 copy.147
  323.8 7.3 %all-to-all-start.6 = ((bf16[1,4,3584]{1,0,2:T(2,128)(2,1)}), bf16[1,4,3584]{1,0,2:T(2,128)(2,1)S(1)}, u32[]{:S(2)}, u32[]{:S(2)}) async-start(bf16[1,4,3584]{1,0,2:T(2,128)(2,1)} %copy.130), calls=%async_computation.6 | async-start | bytes 3670016 | tf_op jit(solution)/shard_map/all_to_all | solution.py:167
  331.1 2.0 slice_convert_fusion
  333.1 3.2 copy.113
  336.3 0.7 reduce_sum.58
  337.7 38.8 %all-to-all-done.6 = bf16[1,4,3584]{1,0,2:T(2,128)(2,1)S(1)} async-done(((bf16[1,4,3584]{1,0,2:T(2,128)(2,1)}), bf16[1,4,3584]{1,0,2:T(2,128)(2,1)S(1)}, u32[]{:S(2)}, u32[]{:S(2)}) %all-to-all-start.6) | async-done | bytes 28704 | tf_op jit(solution)/shard_map/all_to_all | solution.py:167
  376.5 6.2 %all-to-all-start = ((bf16[1,3584,4]{2,0,1:T(2,128)(2,1)}), bf16[1,3584,4]{2,0,1:T(2,128)(2,1)}, u32[]{:S(2)}, u32[]{:S(2)}) async-start(bf16[1,3584,4]{2,0,1:T(2,128)(2,1)} %copy.113), calls=%async_computation | async-start | bytes 3670016 | tf_op jit(solution)/shard_map/all_to_all | solution.py:166
  384.0 44.0 %all-to-all-done = bf16[1,3584,4]{2,0,1:T(2,128)(2,1)} async-done(((bf16[1,3584,4]{2,0,1:T(2,128)(2,1)}), bf16[1,3584,4]{2,0,1:T(2,128)(2,1)}, u32[]{:S(2)}, u32[]{:S(2)}) %all-to-all-start) | async-done | bytes 28704 | tf_op jit(solution)/shard_map/all_to_all | solution.py:166
  428.6 6.0 %all-to-all-start.5 = ((f32[64,1,1]{2,1,0:T(1,128)}), f32[64,1,1]{2,1,0:T(1,128)S(1)}, u32[]{:S(2)}, u32[]{:S(2)}) async-start(f32[64,1,1]{2,1,0:T(1,128)} %broadcast_in_dim.36), calls=%async_computation.5 | async-start | bytes 65536 | tf_op jit(solution)/shard_map/all_to_all | solution.py:52
  434.6 1.8 copy.128
  436.4 1.3 reshape.302
  437.7 1.8 copy.131
  439.8 3.7 copy.114
  444.4 1.6 multiply_bitcast_fusion
  446.0 2.9 copy.129
  448.9 1.5 reshape.303
  450.5 1.1 convolution_multiply_fusion.3
  451.7 1.1 convolution_multiply_fusion.2
  (55 shorter events, 6.7 us)
Async XLA Ops:
  7.2 135.9 %copy-start = (bf16[256,3584]{1,0:T(8,128)(2,1)S(1)}, bf16[256,3584]{1,0:T(8,128)(2,1)}, u32[]{:S(2)}) copy-start(bf16[256,3584]{1,0:T(8,128)(2,1)} %param.11) | copy-start | bytes 5505028
  7.2 135.2 %all-gather.5.cloned.1.call-start = ((), (), s32[]{:S(2)}) async-start(), calls=%async_computation.7 | async-start | bytes 3612672 | tf_op jit(solution)/shard_map/all_gather | solution.py:28
  24.3 185.5 %all-to-all-start.1 = ((bf16[64,896,56]{1,2,0:T(8,128)(2,1)}), bf16[64,896,56]{1,2,0:T(8,128)(2,1)}, u32[]{:S(2)}, u32[]{:S(2)}) async-start(bf16[64,896,56]{1,2,0:T(8,128)(2,1)} %stack.2), calls=%async_computation.1 | async-start | bytes 12845056 | tf_op jit(solution)/shard_map/all_to_all | solution.py:149
  37.8 105.3 %copy-start.4 = (bf16[3584,128]{1,0:T(8,128)(2,1)S(1)}, bf16[3584,128]{1,0:T(8,128)(2,1)}, u32[]{:S(2)}) copy-start(bf16[3584,128]{1,0:T(8,128)(2,1)} %param.14) | copy-start | bytes 2752516
  37.8 131.0 %all-gather.7.cloned.1.call-start = ((), (), s32[]{:S(2)}) async-start(), calls=%async_computation.8 | async-start | bytes 9633792 | tf_op jit(solution)/shard_map/all_gather | solution.py:28
  172.2 2.2 copy-start.9
  172.2 2.2 copy-start.11
  181.5 1.4 copy-start.6
  181.5 1.4 copy-start.7
  183.6 1.2 copy-start.2
  183.6 1.8 copy-start.13
  185.5 2.6 copy-start.12
  209.8 5.0 %copy-start.8 = (bf16[1,4,3584]{2,1,0:T(4,128)(2,1)S(1)}, bf16[1,4,3584]{2,1,0:T(4,128)(2,1)}, u32[]{:S(2)}) copy-start(bf16[1,4,3584]{2,1,0:T(4,128)(2,1)} %param.20) | copy-start | bytes 86020
  222.7 27.0 %all-to-all-start.2 = ((bf16[4,1,256,896]{3,2,1,0:T(8,128)(2,1)}), bf16[4,1,256,896]{3,2,1,0:T(8,128)(2,1)S(1)}, u32[]{:S(2)}, u32[]{:S(2)}) async-start(bf16[4,1,256,896]{3,2,1,0:T(8,128)(2,1)} %bitcast.101), calls=%async_computation.2 | async-start | bytes 3670016 | tf_op jit(solution)/shard_map/all_to_all | solution.py:46
  226.7 23.2 %copy-start.5 = (bf16[256,896]{1,0:T(8,128)(2,1)S(1)}, bf16[256,896]{1,0:T(8,128)(2,1)}, u32[]{:S(2)}) copy-start(bf16[256,896]{1,0:T(8,128)(2,1)} %param.12) | copy-start | bytes 1376260
  259.8 64.1 %all-to-all-start.4 = ((f32[64,1,1]{2,1,0:T(1,128)}), f32[64,1,1]{2,1,0:T(1,128)S(1)}, u32[]{:S(2)}, u32[]{:S(2)}) async-start(f32[64,1,1]{2,1,0:T(1,128)} %broadcast_in_dim.35), calls=%async_computation.4 | async-start | bytes 65536 | tf_op jit(solution)/shard_map/all_to_all | solution.py:52
  323.8 52.6 %all-to-all-start.6 = ((bf16[1,4,3584]{1,0,2:T(2,128)(2,1)}), bf16[1,4,3584]{1,0,2:T(2,128)(2,1)S(1)}, u32[]{:S(2)}, u32[]{:S(2)}) async-start(bf16[1,4,3584]{1,0,2:T(2,128)(2,1)} %copy.130), calls=%async_computation.6 | async-start | bytes 3670016 | tf_op jit(solution)/shard_map/all_to_all | solution.py:167
  331.1 2.0 copy-start.10
  376.5 51.5 %all-to-all-start = ((bf16[1,3584,4]{2,0,1:T(2,128)(2,1)}), bf16[1,3584,4]{2,0,1:T(2,128)(2,1)}, u32[]{:S(2)}, u32[]{:S(2)}) async-start(bf16[1,3584,4]{2,0,1:T(2,128)(2,1)} %copy.113), calls=%async_computation | async-start | bytes 3670016 | tf_op jit(solution)/shard_map/all_to_all | solution.py:166
  428.6 15.3 %all-to-all-start.5 = ((f32[64,1,1]{2,1,0:T(1,128)}), f32[64,1,1]{2,1,0:T(1,128)S(1)}, u32[]{:S(2)}, u32[]{:S(2)}) async-start(f32[64,1,1]{2,1,0:T(1,128)} %broadcast_in_dim.36), calls=%async_computation.5 | async-start | bytes 65536 | tf_op jit(solution)/shard_map/all_to_all | solution.py:52
  439.5 4.9 %copy-start.3 = (f32[64,3584]{0,1:T(8,128)S(1)}, f32[64,3584]{0,1:T(8,128)}, u32[]{:S(2)}) copy-start(f32[64,3584]{0,1:T(8,128)} %copy.128) | copy-start | bytes 2752516
  446.0 6.7 %copy-start.1 = (bf16[256,3584]{1,0:T(8,128)(2,1)S(1)}, bf16[256,3584]{1,0:T(8,128)(2,1)}, u32[]{:S(2)}) copy-start(bf16[256,3584]{1,0:T(8,128)(2,1)} %param.11) | copy-start | bytes 5505028
Sparse Core Ops, SparseCore 0:
  20.4 121.9 all-gather.4
  144.1 24.6 all-gather.6
